TPU v7x, 32 devices: a whole 2x2x4 slice. The times are simulated.
32 devices in a mesh: win: 2 (over y), row: 16 (over z, x, core).
Axes of the slice: x: 2, y: 2, z: 4, core: 2. Of those that a mesh axis runs over, the one named last changes fastest.
Arguments:
- spectra: bfloat16 [32, 2, 32768], P(('win', 'row')), parts along dimension 0, may hold values from -6 to 6
- pair_mask: int32 [16, 16], P('row'), may hold values from 0 to 1, as said below
- available: int32 [32], P('win'), parts along dimension 0, may hold values 0 or 1
Outputs:
- correlations: float32 [32, 16, 8192], P(('win', 'row')), parts along dimension 0
There are 2 independent parts, one for each index of `win`. A program takes and returns all parts, laid end to end along the dimension named above; an argument that names none is the same for every part. Nothing has to cross between parts.
Inputs may be any that keep to these rules, and one draw needn't show every extreme that they name: pair_mask[i, j] is 0 wherever j <= i.
All inputs are finite; a program needn't handle non-finite values.
Results may differ from a plain program's by a relative error of at most 0.0003.
Values may be sent and summed in bfloat16 or wider, within the bound.
A program may use at most 128 MiB of HBM per device.

v0:
```python
import math

import jax
import jax.numpy as jnp
from jax import lax
from jax.sharding import PartitionSpec as P

LAGS = 8192


full_turn = 2.0 * math.pi


def shifted(value, axis, by):
    size = lax.axis_size(axis)
    return lax.ppermute(value, axis, [(i, (i + by) % size) for i in range(size)])


def build_tables(freq, lags):
    nfft = 2 * freq
    inner = min(128, lags // 2)
    column = nfft // inner
    depth = freq // column
    outer = lags // inner
    centre = lags // 2
    t_inner = jnp.arange(inner, dtype=jnp.int32)
    k_depth = jnp.arange(depth, dtype=jnp.int32)
    k_column = jnp.arange(column, dtype=jnp.int32)
    t_outer = jnp.arange(outer, dtype=jnp.int32)
    first = full_turn * (t_inner[:, None] * k_depth[None, :] % inner).astype(jnp.float32) / inner
    cos_first = jnp.cos(first)
    sin_first = jnp.sin(first)
    section_one = jnp.concatenate(
        [
            jnp.concatenate([cos_first, -sin_first], axis=1),
            jnp.concatenate([sin_first, cos_first], axis=1),
        ],
        axis=0,
    )
    twist = (
        full_turn
        * jnp.mod(k_column[None, :] * (t_inner[:, None] - centre), nfft).astype(jnp.float32)
        / nfft
    )
    second = (
        full_turn * (t_outer[:, None] * k_column[None, :] % column).astype(jnp.float32) / column
    )
    section_two = jnp.stack([jnp.cos(second), -jnp.sin(second)], axis=1)
    return (section_one, jnp.cos(twist), jnp.sin(twist), section_two)


def pair_block(own_wide, part, signs, tables):
    section_one, twist_cos, twist_sin, section_two = tables
    count = own_wide.shape[0]
    width = part.shape[0]
    freq = part.shape[2]
    inner = twist_cos.shape[0]
    column = twist_cos.shape[1]
    outer = section_two.shape[0]
    depth = freq // column
    other = part.astype(jnp.float32)
    real_part = (
        own_wide[:, None, 0, :] * other[None, :, 0, :]
        + own_wide[:, None, 1, :] * other[None, :, 1, :]
    )
    imag_part = (
        own_wide[:, None, 0, :] * other[None, :, 1, :]
        - own_wide[:, None, 1, :] * other[None, :, 0, :]
    ) * signs[:, :, None]
    cross = jnp.stack([real_part, imag_part], axis=2).reshape(count * width, 2 * depth, column)
    mixed = jnp.einsum("uv,pvk->puk", section_one, cross, precision=lax.Precision.HIGH)
    mixed = mixed.reshape(count * width, 2, inner, column)
    turned_real = mixed[:, 0] * twist_cos - mixed[:, 1] * twist_sin
    turned_imag = mixed[:, 0] * twist_sin + mixed[:, 1] * twist_cos
    turned = jnp.stack([turned_real, turned_imag], axis=1)
    summed = jnp.einsum("tck,pcuk->ptu", section_two, turned, precision=lax.Precision.HIGH)
    summed = summed.reshape(count, width, outer * inner)
    return (2.0 * summed - real_part[:, :, :1]) * (1.0 / math.sqrt(8.0 * freq))


def correlate(own, others, signs, tables):
    own_wide = own.astype(jnp.float32)
    count = own.shape[0]
    total = others.shape[0]
    width = math.gcd(total, max(1, 8 // count))
    if width == total:
        return pair_block(own_wide, others, signs, tables)
    groups = total // width
    pieces = others.reshape(groups, width, 2, others.shape[2])
    sign_pieces = jnp.transpose(signs.reshape(count, groups, width), (1, 0, 2))

    def one_group(item):
        return pair_block(own_wide, item[0], item[1], tables)

    results = lax.map(one_group, (pieces, sign_pieces))
    return jnp.transpose(results, (1, 0, 2, 3)).reshape(count, total, results.shape[3])


def per_device(spectra, pair_mask, available):
    count = spectra.shape[0]
    devices = lax.axis_size("row")
    stations = count * devices
    freq = spectra.shape[2]
    tables = build_tables(freq, LAGS)
    first_station = lax.axis_index("row") * count
    own_flags = lax.dynamic_slice_in_dim(available, first_station, count, 0).astype(jnp.float32)
    weight = (
        pair_mask.astype(jnp.float32) * own_flags[:, None] * available.astype(jnp.float32)[None, :]
    )
    reach = devices // 2 + 1
    window = spectra
    have = 1
    while have < reach:
        take = min(have, reach - have)
        moved = shifted(window[: take * count], "row", -have)
        window = jnp.concatenate([window, moved], axis=0)
        have = have + take
    half = stations // 2
    offsets = jnp.arange(half, dtype=jnp.int32) + 1
    columns = jnp.arange(stations, dtype=jnp.int32)
    station = first_station + 0
    signs = jnp.where(station + offsets >= stations, -1.0, 1.0).astype(jnp.float32)[None, :]
    near = correlate(window[0:1], window[1 : 1 + half], signs, tables)[0]
    padded = jnp.concatenate([near, jnp.zeros_like(near)], axis=0)
    placed = jnp.roll(padded, station + 1, axis=0)
    keep_rows = [jnp.where((columns > station)[:, None], placed, 0.0)]
    send_rows = [jnp.where((columns < station - half)[:, None], placed, 0.0)]
    kept = jnp.stack(keep_rows, axis=0)
    outgoing = jnp.stack(send_rows, axis=1)
    incoming = lax.all_to_all(outgoing, "row", split_axis=0, concat_axis=1, tiled=True)
    corr = kept + incoming
    return corr * weight[:, :, None]


def solution(mesh):
    return jax.shard_map(
        per_device,
        mesh=mesh,
        in_specs=(P(("win", "row"), None, None), P("row", None), P("win")),
        out_specs=P(("win", "row"), None, None),
        check_vma=False,
    )
```

profile of v0, /device:TPU:1, one launch (start us, length us, event | category | flops | bytes accessed | tf_op | source)
XLA Modules:
  0.0 77.0 jit_solution(7756633121859793812)
XLA Ops:
  0.0 0.0 collective-permute-start
  0.0 3.8 %collective-permute-start.3 = (bf16[1,2,32768]{2,1,0:T(2,128)(2,1)}, bf16[1,2,32768]{2,1,0:T(2,128)(2,1)S(1)}, u32[]{:S(2)}, u32[]{:S(2)}) collective-permute-start(bf16[1,2,32768]{2,1,0:T(2,128)(2,1)} %param.3), channel_id=1, source_target_pairs={{0,8},{1,9},{2,10},{3,11},{4,12},{5,13},{6,14},{7,15},{8,0},{9,1},... | collective-permute-start | bytes 393224 | tf_op jit(solution)/shard_map/ppermute | solution.py:16
  3.8 1.2 %fusion.60 = (f32[1,1,32768]{2,1,0:T(1,128)S(1)}, f32[1,1,32768]{2,1,0:T(1,128)S(1)}) fusion(bf16[1,2,32768]{2,1,0:T(2,128)(2,1)} %param.3), kind=kLoop, calls=%fused_computation.92 | loop fusion | bytes 524288 | tf_op jit(solution)/shard_map/slice | solution.py:63
  5.0 0.4 collective-permute-done
  5.5 1.3 %pad_maximum_fusion.2 = bf16[2,2,32768]{2,1,0:T(2,128)(2,1)S(1)} fusion(bf16[1,2,32768]{2,1,0:T(2,128)(2,1)S(1)} %collective-permute-done, bf16[1,2,32768]{2,1,0:T(2,128)(2,1)} %param.3), kind=kLoop, calls=%fused_computation.37 | loop fusion | flops 131072 | bytes 524288 | tf_op jit(solution)/shard_map/concatenate | solution.py:116
  6.7 7.0 %collective-permute-start.1 = (bf16[2,2,32768]{2,1,0:T(2,128)(2,1)S(1)}, bf16[2,2,32768]{2,1,0:T(2,128)(2,1)S(1)}, u32[]{:S(2)}, u32[]{:S(2)}) collective-permute-start(bf16[2,2,32768]{2,1,0:T(2,128)(2,1)S(1)} %pad_maximum_fusion.2), channel_id=1, source_target_pairs={{0,14},{1,15},{2,0},{3,1},{4,2},{5,3},{6,4},{7,5},{8,6},{9,7},{10,... | collective-permute-start | bytes 786440 | tf_op jit(solution)/shard_map/ppermute | solution.py:16
  13.7 0.9 %fusion.54 = f32[128,64]{1,0:T(8,128)} fusion(), kind=kLoop, calls=%fused_computation.79 | loop fusion | flops 122880 | bytes 32768 | tf_op jit(solution)/shard_map/neg | solution.py:35
  14.6 0.9 %fusion.52 = (f32[128,64]{1,0:T(8,128)}, f32[128,64]{1,0:T(8,128)}) fusion(), kind=kLoop, calls=%fused_computation.77 | loop fusion | flops 114688 | bytes 65536 | tf_op jit(solution)/shard_map/sin | solution.py:32
  15.5 1.5 %collective-permute-done.1 = bf16[2,2,32768]{2,1,0:T(2,128)(2,1)S(1)} collective-permute-done((bf16[2,2,32768]{2,1,0:T(2,128)(2,1)S(1)}, bf16[2,2,32768]{2,1,0:T(2,128)(2,1)S(1)}, u32[]{:S(2)}, u32[]{:S(2)}) %collective-permute-start.1) | collective-permute-done | bytes 262176 | tf_op jit(solution)/shard_map/ppermute | solution.py:16
  17.0 1.7 %pad_maximum_fusion.1 = bf16[4,2,32768]{2,1,0:T(2,128)(2,1)S(1)} fusion(bf16[2,2,32768]{2,1,0:T(2,128)(2,1)S(1)} %collective-permute-done.1, bf16[1,2,32768]{2,1,0:T(2,128)(2,1)S(1)} %collective-permute-done, bf16[1,2,32768]{2,1,0:T(2,128)(2,1)} %param.3), kind=kLoop, calls=%fused_computation.25 | loop fusion | flops 524288 | bytes 1048576 | tf_op jit(solution)/shard_map/concatenate | solution.py:116
  18.7 2.1 %collective-permute-start.2 = (bf16[4,2,32768]{2,1,0:T(2,128)(2,1)S(1)}, bf16[4,2,32768]{2,1,0:T(2,128)(2,1)S(1)}, u32[]{:S(2)}, u32[]{:S(2)}) collective-permute-start(bf16[4,2,32768]{2,1,0:T(2,128)(2,1)S(1)} %pad_maximum_fusion.1), channel_id=1, source_target_pairs={{0,12},{1,13},{2,14},{3,15},{4,0},{5,1},{6,2},{7,3},{8,4},{9,5},{1... | collective-permute-start | bytes 1572872 | tf_op jit(solution)/shard_map/ppermute | solution.py:16
  20.8 1.9 %fusion.43 = (f32[128,512]{1,0:T(8,128)S(1)}, f32[128,512]{1,0:T(8,128)}) fusion(s32[128]{0:T(128)S(1)} %iota_add_fusion), kind=kLoop, calls=%fused_computation.63 | loop fusion | flops 917504 | bytes 524800 | tf_op jit(solution)/shard_map/cos | solution.py:49
  22.6 0.6 slice.42
  23.2 0.5 slice.44
  23.7 1.2 %sine_negate_fusion = (f32[64,1,512]{2,0,1:T(8,128)S(1)}, f32[64,1,512]{2,0,1:T(8,128)}) fusion(), kind=kLoop, calls=%fused_computation.59 | loop fusion | flops 491520 | bytes 262144 | tf_op jit(solution)/shard_map/neg | solution.py:48
  24.9 6.8 %collective-permute-done.2 = bf16[4,2,32768]{2,1,0:T(2,128)(2,1)S(1)} collective-permute-done((bf16[4,2,32768]{2,1,0:T(2,128)(2,1)S(1)}, bf16[4,2,32768]{2,1,0:T(2,128)(2,1)S(1)}, u32[]{:S(2)}, u32[]{:S(2)}) %collective-permute-start.2) | collective-permute-done | bytes 524320 | tf_op jit(solution)/shard_map/ppermute | solution.py:16
  31.7 1.4 %maximum_convert_fusion = f32[8,2,32768]{2,1,0:T(2,128)S(1)} fusion(bf16[1,2,32768]{2,1,0:T(2,128)(2,1)S(1)} %collective-permute-done.3, bf16[4,2,32768]{2,1,0:T(2,128)(2,1)S(1)} %collective-permute-done.2, bf16[2,2,32768]{2,1,0:T(2,128)(2,1)S(1)} %collective-permute-done.1, bf16[1,2,32768]{2,1,0:T(2,128)(2,1)S(1)} %collective-permute-done), kind=kLoop, calls=%fused_computation.10 | loop fusion | flops 2097152 | bytes 3145728 | tf_op jit(solution)/shard_map/convert_element_type | solution.py:61
  33.1 3.0 %slice_bitcast_fusion.1 = (f32[1,8,32768]{2,0,1:T(1,128)S(1)}, f32[1,8,32768]{2,0,1:T(1,128)}) fusion(f32[8,2,32768]{2,1,0:T(2,128)S(1)} %maximum_convert_fusion), kind=kLoop, calls=%fused_computation.76 | loop fusion | bytes 4194304 | tf_op jit(solution)/shard_map/broadcast_in_dim;squeeze | solution.py:63
  36.1 2.6 %fusion.13 = (f32[1,8,1,32768]{3,2,1,0:T(1,128)S(1)}, f32[1,8,1,32768]{3,2,1,0:T(1,128)S(1)}) fusion(f32[32768]{0:T(1024)S(1)} %bitcast.65, f32[32768]{0:T(1024)S(1)} %bitcast.63, f32[8,2,32768]{2,1,0:T(2,128)S(1)} %maximum_convert_fusion, f32[8]{0:T(128)S(1)} %compare_select_fusion), kind=kLoop, calls=%fused_computation.17 | loop fusion | flops 1835008 | bytes 4456480 | tf_op jit(solution)/shard_map/add | solution.py:63
  38.7 3.2 %pad_maximum_fusion = f32[1,8,2,32768]{3,2,1,0:T(2,128)} fusion(f32[1,8,1,32768]{3,2,1,0:T(1,128)S(1)} %get-tuple-element.8, f32[1,8,1,32768]{3,2,1,0:T(1,128)S(1)} %get-tuple-element.7), kind=kLoop, calls=%fused_computation.4 | loop fusion | flops 524288 | bytes 4194304 | tf_op jit(solution)/shard_map/stack | solution.py:70
  41.9 3.2 %reshape.460 = f32[8,128,512]{2,1,0:T(8,128)S(1)} reshape(f32[1,8,2,32768]{3,2,1,0:T(2,128)} %pad_maximum_fusion) | data formatting | bytes 4194304 | tf_op jit(solution)/shard_map/reshape | solution.py:70
  45.2 3.2 %fusion.33 = f32[8,512,256]{1,2,0:T(8,128)S(1)} fusion(f32[8,128,512]{2,1,0:T(8,128)S(1)} %reshape.460, f32[128,64]{1,0:T(8,128)} %get-tuple-element.16, f32[128,64]{1,0:T(8,128)} %get-tuple-element.15, f32[128,64]{1,0:T(8,128)} %fusion.54), kind=kOutput, calls=%fused_computation.52 | convolution fusion | flops 805404672 | bytes 6389760 | tf_op jit(solution)/shard_map/uv,pvk->puk/dot_general | solution.py:71
  48.4 0.7 multiply_subtract_fusion
  49.1 2.1 %fusion.56 = f32[8]{0:T(128)S(1)} fusion(f32[1,8,32768]{2,0,1:T(1,128)} %get-tuple-element.10, f32[1,8,32768]{2,0,1:T(1,128)S(1)} %get-tuple-element.9, f32[1]{0:T(128)} %slice.44, f32[1]{0:T(128)} %slice.42), kind=kLoop, calls=%fused_computation.83 | loop fusion | flops 24 | bytes 104 | tf_op jit(solution)/shard_map/slice | solution.py:78
  51.2 2.0 %fusion.10 = f32[1,8,64,128]{3,2,1,0:T(8,128)S(1)} fusion(f32[8,1,128,512]{3,2,1,0:T(8,128)S(1)} %get-tuple-element.6, f32[8,1,128,512]{3,2,1,0:T(8,128)S(1)} %get-tuple-element.5, f32[64,1,512]{2,0,1:T(8,128)S(1)} %get-tuple-element.17, f32[64,1,512]{2,0,1:T(8,128)S(1)} %copy-done.1), kind=kOutput, calls=%fused_computation.9 | convolution fusion | flops 403832832 | bytes 4718592 | tf_op jit(solution)/shard_map/tck,pcuk->ptu/dot_general | solution.py:76
  53.2 0.2 fusion.24
  53.4 0.3 broadcast_select_fusion
  53.7 1.3 %stack.22 = f32[16,1,8192]{2,1,0:T(1,128)} reshape(f32[16,8192]{1,0:T(8,128)S(1)} %broadcast_select_fusion) | data formatting | bytes 1048576 | tf_op jit(solution)/shard_map/stack | solution.py:129
  55.0 6.7 %all-to-all-start = ((f32[16,1,8192]{2,1,0:T(1,128)}), f32[16,1,8192]{2,1,0:T(1,128)S(1)}, u32[]{:S(2)}, u32[]{:S(2)}) async-start(f32[16,1,8192]{2,1,0:T(1,128)} %stack.22), calls=%async_computation | async-start | bytes 1048576 | tf_op jit(solution)/shard_map/all_to_all | solution.py:130
  61.7 0.6 dynamic_slice.8
  63.0 12.7 %all-to-all-done = f32[16,1,8192]{2,1,0:T(1,128)S(1)} async-done(((f32[16,1,8192]{2,1,0:T(1,128)}), f32[16,1,8192]{2,1,0:T(1,128)S(1)}, u32[]{:S(2)}, u32[]{:S(2)}) %all-to-all-start) | async-done | bytes 524320 | tf_op jit(solution)/shard_map/all_to_all | solution.py:130
  75.7 1.2 %fusion.20 = f32[1,16,8192]{2,1,0:T(8,128)} fusion(f32[16,1,8192]{2,1,0:T(1,128)S(1)} %all-to-all-done, f32[16]{0:T(128)S(1)} %fusion.57, pred[16]{0:T(512)(128)(4,1)S(1)} %iota_compare_fusion.1, s32[]{:T(128)S(6)} %select_n.86, f32[8,8192]{1,0:T(8,128)S(1)} %broadcast_in_dim.49, f32[8,8192]{1,0:T(8,128)S(1)} %fusion.24), kind=kLoop, calls=%fused_computation.28 | loop fusion | flops 786432 | bytes 1572948 | tf_op jit(solution)/shard_map/mul | solution.py:132
  (15 shorter events, 0.1 us)
Async XLA Ops:
  0.0 5.5 %collective-permute-start = (bf16[1,2,32768]{2,1,0:T(2,128)(2,1)}, bf16[1,2,32768]{2,1,0:T(2,128)(2,1)S(1)}, u32[]{:S(2)}, u32[]{:S(2)}) collective-permute-start(bf16[1,2,32768]{2,1,0:T(2,128)(2,1)} %param.3), channel_id=1, source_target_pairs={{0,15},{1,0},{2,1},{3,2},{4,3},{5,4},{6,5},{7,6},{8,7},{9,8},{10,9... | collective-permute-start | bytes 393224 | tf_op jit(solution)/shard_map/ppermute | solution.py:16
  0.0 24.9 %collective-permute-start.3 = (bf16[1,2,32768]{2,1,0:T(2,128)(2,1)}, bf16[1,2,32768]{2,1,0:T(2,128)(2,1)S(1)}, u32[]{:S(2)}, u32[]{:S(2)}) collective-permute-start(bf16[1,2,32768]{2,1,0:T(2,128)(2,1)} %param.3), channel_id=1, source_target_pairs={{0,8},{1,9},{2,10},{3,11},{4,12},{5,13},{6,14},{7,15},{8,0},{9,1},... | collective-permute-start | bytes 393224 | tf_op jit(solution)/shard_map/ppermute | solution.py:16
  6.7 10.3 %collective-permute-start.1 = (bf16[2,2,32768]{2,1,0:T(2,128)(2,1)S(1)}, bf16[2,2,32768]{2,1,0:T(2,128)(2,1)S(1)}, u32[]{:S(2)}, u32[]{:S(2)}) collective-permute-start(bf16[2,2,32768]{2,1,0:T(2,128)(2,1)S(1)} %pad_maximum_fusion.2), channel_id=1, source_target_pairs={{0,14},{1,15},{2,0},{3,1},{4,2},{5,3},{6,4},{7,5},{8,6},{9,7},{10,... | collective-permute-start | bytes 786440 | tf_op jit(solution)/shard_map/ppermute | solution.py:16
  18.7 13.0 %collective-permute-start.2 = (bf16[4,2,32768]{2,1,0:T(2,128)(2,1)S(1)}, bf16[4,2,32768]{2,1,0:T(2,128)(2,1)S(1)}, u32[]{:S(2)}, u32[]{:S(2)}) collective-permute-start(bf16[4,2,32768]{2,1,0:T(2,128)(2,1)S(1)} %pad_maximum_fusion.1), channel_id=1, source_target_pairs={{0,12},{1,13},{2,14},{3,15},{4,0},{5,1},{6,2},{7,3},{8,4},{9,5},{1... | collective-permute-start | bytes 1572872 | tf_op jit(solution)/shard_map/ppermute | solution.py:16
  45.2 3.2 %copy-start = (f32[128,512]{1,0:T(8,128)S(1)}, f32[128,512]{1,0:T(8,128)}, u32[]{:S(2)}) copy-start(f32[128,512]{1,0:T(8,128)} %get-tuple-element.14) | copy-start | bytes 786436
  48.4 2.8 %copy-start.1 = (f32[64,1,512]{2,0,1:T(8,128)S(1)}, f32[64,1,512]{2,0,1:T(8,128)}, u32[]{:S(2)}) copy-start(f32[64,1,512]{2,0,1:T(8,128)} %get-tuple-element.18) | copy-start | bytes 393220
  53.2 8.5 %copy-start.2 = (s32[16]{0:T(128)S(1)}, s32[16]{0:T(128)}, u32[]{:S(2)}) copy-start(s32[16]{0:T(128)} %param.5) | copy-start | bytes 196
  53.2 9.8 %copy-start.3 = (s32[1,16]{1,0:T(1,128)S(1)}, s32[1,16]{1,0:T(1,128)}, u32[]{:S(2)}) copy-start(s32[1,16]{1,0:T(1,128)} %param.4) | copy-start | bytes 196
  55.0 20.7 %all-to-all-start = ((f32[16,1,8192]{2,1,0:T(1,128)}), f32[16,1,8192]{2,1,0:T(1,128)S(1)}, u32[]{:S(2)}, u32[]{:S(2)}) async-start(f32[16,1,8192]{2,1,0:T(1,128)} %stack.22), calls=%async_computation | async-start | bytes 1048576 | tf_op jit(solution)/shard_map/all_to_all | solution.py:130
where the time goes:
time: 77.7 us; the launch traced here: 77 us
  waiting for transfers between devices  21.4 us (28%)
  starting transfers between devices  19.5 us (25%)
  other arithmetic  19.5 us (25%)
  local copies, waits for them, and re-layouts  10.5 us (14%)
  matrix products  5.22 us (7%)
  between operations  0.78 us (1%)
    ppermute x4, starting transfers between devices, shifted(): lax.ppermute(value, axis, [(i, (i + by) % size) for i in range(size)])  12.8 us
    all_to_all x1, waiting for transfers between devices, per_device(): lax.all_to_all(outgoing, 'row', split_axis=0, concat_axis=1, tiled=True)  12.7 us
    ppermute x4, waiting for transfers between devices, shifted(): lax.ppermute(value, axis, [(i, (i + by) % size) for i in range(size)])  8.73 us
    all_to_all x1, starting transfers between devices, per_device(): lax.all_to_all(outgoing, 'row', split_axis=0, concat_axis=1, tiled=True)  6.7 us
    reshape x1, local copies, waits for them, and re-layouts, pair_block(): jnp.stack([real_part, imag_part], axis=2)  3.23 us
    another operation x1, other arithmetic, pair_block(): jnp.stack([real_part, imag_part], axis=2)  3.2 us
    dot_general x1, matrix products, pair_block(): jnp.einsum('uv,pvk->puk', section_one, cross, precision=lax.Precision.HIGH)  3.2 us
    another operation x1, local copies, waits for them, and re-layouts, pair_block(): other[None, :, 0, :]  2.99 us
  transfers between devices with their start and end apart: 5, of which 4 were waited for; matrix products, arithmetic and copies ran while one was open for 14% of the time, Pallas kernels for 0%

commit v1 on v0

v1 whole, which is shorter than its diff:
```python
import functools
import math

import jax
import jax.numpy as jnp
import numpy as np
from jax import lax
from jax.experimental import pallas as pl
from jax.experimental.pallas import tpu as pltpu
from jax.sharding import PartitionSpec as P

LAGS = 8192
MESH = pl.DeviceIdType.MESH
PIECES = 2
LINE = 2
CORES = 2


def split(value):
    high = value.astype(jnp.bfloat16)
    low = (value - high.astype(jnp.float32)).astype(jnp.bfloat16)
    return high, low


def build_tables(freq, lags):
    nfft = 2 * freq
    inner = min(128, lags // 2)
    column = nfft // inner
    depth = freq // column
    outer = lags // inner
    centre = lags // 2
    turn = 2.0 * np.pi
    t_inner = np.arange(inner)[:, None]
    first = turn * ((t_inner * np.arange(depth)[None, :]) % inner) / inner
    cos_first, sin_first = np.cos(first), np.sin(first)
    one = np.block([[cos_first, -sin_first], [sin_first, cos_first]]).astype(np.float32)
    k_column = np.arange(column)[None, :]
    twist = turn * ((k_column * (t_inner - centre)) % nfft) / nfft
    second = turn * ((np.arange(outer)[:, None] * k_column) % column) / column
    two = np.concatenate([np.cos(second), -np.sin(second)], axis=1).astype(np.float32)

    def halves(table):
        high = table.astype(jnp.bfloat16)
        low = (table - high.astype(np.float32)).astype(jnp.bfloat16)
        return high, low

    one_high, one_low = halves(one)
    two_high, two_low = halves(two)
    return (
        np.concatenate([one_high, one_high, one_low], axis=1),
        np.stack([np.cos(twist), np.sin(twist)]).astype(np.float32),
        np.concatenate([two_high, two_low], axis=0),
    )


def kernel(
    devices,
    mask_ref,
    avail_ref,
    x_ref,
    one_ref,
    twist_ref,
    two_ref,
    out_ref,
    buf,
    own,
    res,
    recv,
    send_z,
    send_x,
    send_d,
):
    planes = devices // (LINE * CORES)
    me = lax.axis_index("row")
    core = me % CORES
    chip = me // CORES
    side = chip % LINE
    plane = chip // LINE
    depth = x_ref.shape[1]
    inner = twist_ref.shape[1]
    outer = two_ref.shape[0] // 2
    freq = depth * x_ref.shape[2]
    scale = 2.0 / math.sqrt(8.0 * freq)
    rows = depth // PIECES

    def index(p, s, c):
        return (p * LINE + s) * CORES + c

    below = index(plane - 1, side, core)
    above = index(plane + 1, side, core)
    beside = index(plane, 1 - side, core)
    twin = index(plane, side, 1 - core)

    def greet(device):
        pl.semaphore_signal(barrier, inc=1, device_id={"row": device}, device_id_type=MESH)

    def piece(ref, k):
        return ref.at[:, pl.ds(k * rows, rows), :]

    def copy(station, p, k, sem, kind, device, mine=False):
        slot = piece(buf.at[station], k)
        return pltpu.make_async_remote_copy(
            src_ref=piece(x_ref, k) if mine else slot,
            dst_ref=slot,
            send_sem=sem,
            recv_sem=recv.at[kind, p, k],
            device_id={"row": device},
            device_id_type=MESH,
        )

    def down(p, k, mine=False):
        return copy(index(p, side, core), p, k, send_z.at[p, k], 0, below, mine)

    def across(p, k, mine=False):
        return copy(index(p, side, core), p, k, send_x.at[p, k], 1, beside, mine)

    def over(p, k, mine=False):
        return copy(index(p, side, core), p, k, send_d.at[0, p, k], 2, twin, mine)

    def over_side(p, k):
        return copy(index(p, 1 - side, core), p, k, send_d.at[1, p, k], 3, twin)

    def arrived(station, p, k, kind):
        slot = piece(buf.at[station], k)
        pltpu.make_async_remote_copy(
            src_ref=slot,
            dst_ref=slot,
            send_sem=send_z.at[p, k],
            recv_sem=recv.at[kind, p, k],
            device_id={"row": twin},
            device_id_type=MESH,
        ).wait_recv()

    barrier = pltpu.get_barrier_semaphore()
    greet(beside)
    greet(twin)

    @pl.when(plane > 0)
    def _():
        greet(below)

    @pl.when(plane < planes - 1)
    def _():
        greet(above)

    first = (
        (lax.broadcasted_iota(jnp.int32, (depth, x_ref.shape[2]), 0) == 0)
        & (lax.broadcasted_iota(jnp.int32, (depth, x_ref.shape[2]), 1) == 0)
    )
    weight = jnp.where(first, 0.5, 1.0)
    own[0] = x_ref[0].astype(jnp.float32) * weight
    own[1] = x_ref[1].astype(jnp.float32) * weight

    peers = 2 + jnp.where(plane > 0, 1, 0) + jnp.where(plane < planes - 1, 1, 0)
    pl.semaphore_wait(barrier, peers)

    for k in range(PIECES):

        @pl.when(plane > 0)
        def _():
            down(plane, k, True).start()

        @pl.when(side == 1)
        def _():
            across(plane, k, True).start()

        @pl.when(core == 1)
        def _():
            over(plane, k, True).start()

    def clear(g, carry):
        res[g] = jnp.zeros(res.shape[1:], jnp.float32)
        return carry

    lax.fori_loop(0, devices, clear, 0)

    def correlate(station):
        own_re, own_im = own[0], own[1]
        re = buf[station, 0].astype(jnp.float32)
        im = buf[station, 1].astype(jnp.float32)
        re_high, re_low = split(own_re * re + own_im * im)
        im_high, im_low = split(own_re * im - own_im * re)
        cross = jnp.concatenate([re_high, im_high, re_low, im_low, re_high, im_high], axis=0)
        mixed = jnp.dot(one_ref[...], cross, preferred_element_type=jnp.float32)
        real, imag = mixed[:inner], mixed[inner:]
        turned_re = real * twist_ref[0] - imag * twist_ref[1]
        turned_im = real * twist_ref[1] + imag * twist_ref[0]
        high, low = split(jnp.concatenate([turned_re, turned_im], axis=1))
        both = jnp.concatenate([high, low], axis=0)
        summed = lax.dot_general(
            two_ref[...],
            both,
            (((1,), (1,)), ((), ())),
            preferred_element_type=jnp.float32,
        )
        total = (summed[:outer, :inner] + summed[:outer, inner:]) + (
            summed[outer:, :inner] + summed[outer:, inner:]
        )
        flag = (mask_ref[0, station] * avail_ref[me] * avail_ref[station]).astype(jnp.float32)
        res[station] = total * (flag * scale)

    def side_in(p):
        for k in range(PIECES):
            arrived(index(p, 1 - side, core), p, k, 1)
            over_side(p, k).start()

    @pl.when(side == 0)
    def _():
        side_in(plane)

    @pl.when(core == 0)
    def _():
        for k in range(PIECES):
            arrived(twin, plane, k, 2)
        correlate(twin)

    @pl.when(side == 0)
    def _():
        correlate(beside)
        for k in range(PIECES):
            arrived(index(plane, 1 - side, 1 - core), plane, k, 3)
        correlate(index(plane, 1 - side, 1 - core))

    def step(p, carry):
        for k in range(PIECES):
            arrived(index(p, side, core), p, k, 0)

            @pl.when(plane > 0)
            def _():
                down(p, k).start()

            across(p, k).start()
            over(p, k).start()
        correlate(index(p, side, core))
        side_in(p)
        for k in range(PIECES):
            arrived(index(p, side, 1 - core), p, k, 2)
        correlate(index(p, side, 1 - core))
        correlate(index(p, 1 - side, core))
        for k in range(PIECES):
            arrived(index(p, 1 - side, 1 - core), p, k, 3)
        correlate(index(p, 1 - side, 1 - core))
        return carry

    lax.fori_loop(plane + 1, planes, step, 0)

    group = math.gcd(devices, 8)

    def place(g, carry):
        at = pl.multiple_of(g * group, group)
        for o in range(outer):
            out_ref[pl.ds(at, group), o * inner : (o + 1) * inner] = res[pl.ds(at, group), o, :]
        return carry

    lax.fori_loop(0, devices // group, place, 0)

    for k in range(PIECES):

        @pl.when(plane > 0)
        def _():
            down(plane, k, True).wait_send()

        @pl.when(side == 1)
        def _():
            across(plane, k, True).wait_send()

        @pl.when(side == 0)
        def _():
            over_side(plane, k).wait_send()

        @pl.when(core == 1)
        def _():
            over(plane, k, True).wait_send()

    def finish(p, carry):
        for k in range(PIECES):

            @pl.when(plane > 0)
            def _():
                down(p, k).wait_send()

            across(p, k).wait_send()
            over(p, k).wait_send()
            over_side(p, k).wait_send()
        return carry

    lax.fori_loop(plane + 1, planes, finish, 0)


def per_device(spectra, pair_mask, available):
    devices = lax.axis_size("row")
    freq = spectra.shape[2]
    one, twist, two = build_tables(freq, LAGS)
    inner, column = twist.shape[1:]
    depth = freq // column
    planes = devices // (LINE * CORES)
    vmem = pl.BlockSpec(memory_space=pltpu.VMEM)
    smem = pl.BlockSpec(memory_space=pltpu.SMEM)
    rows = pl.pallas_call(
        functools.partial(kernel, devices),
        out_shape=jax.ShapeDtypeStruct((devices, LAGS), jnp.float32),
        in_specs=[smem, smem, vmem, vmem, vmem, vmem],
        out_specs=vmem,
        scratch_shapes=[
            pltpu.VMEM((devices, 2, depth, column), jnp.bfloat16),
            pltpu.VMEM((2, depth, column), jnp.float32),
            pltpu.VMEM((devices, LAGS // inner, inner), jnp.float32),
            pltpu.SemaphoreType.DMA((4, planes, PIECES)),
            pltpu.SemaphoreType.DMA((planes, PIECES)),
            pltpu.SemaphoreType.DMA((planes, PIECES)),
            pltpu.SemaphoreType.DMA((2, planes, PIECES)),
        ],
        compiler_params=pltpu.CompilerParams(
            collective_id=0, has_side_effects=True, vmem_limit_bytes=48 * 1024 * 1024
        ),
    )(
        pair_mask,
        available,
        spectra.reshape(2, depth, column),
        jnp.asarray(one),
        jnp.asarray(twist),
        jnp.asarray(two),
    )
    return rows[None]


def solution(mesh):
    return jax.shard_map(
        per_device,
        mesh=mesh,
        in_specs=(P(("win", "row"), None, None), P("row", None), P("win")),
        out_specs=P(("win", "row"), None, None),
        check_vma=False,
    )
```

time: 77.7 us -> 34.3 us (0.44)
  the two profiles are of different devices: /device:TPU:1 before, /device:TPU:3 now
where the time goes in v1:
time: 34.3 us; the launch traced here: 34.1 us
  Pallas kernels  29.6 us (86%)
  local copies, waits for them, and re-layouts  4.39 us (13%)
    pallas_call x1, Pallas kernels, per_device(): pl.pallas_call(functools.partial(kernel, devices), out_shape=jax.ShapeDty...  29.6 us
    unnamed x12, local copies, waits for them, and re-layouts  4.39 us

profile of v1, /device:TPU:3, one launch (start us, length us, event | category | flops | bytes accessed | tf_op | source)
XLA Modules:
  0.0 34.1 jit_solution(4618751228283675046)
XLA Ops:
  0.0 0.0 copy-start.1
  0.0 1.0 %copy.9 = bf16[1,2,64,512]{3,2,1,0:T(8,128)(2,1)S(1)} copy(bf16[1,2,64,512]{3,1,2,0:T(2,128)(2,1)} %bitcast.8) | data formatting | bytes 262144
  1.0 0.0 copy-start.3
  1.0 0.0 copy-start.4
  1.0 0.0 copy-done.1
  1.0 0.6 %copy-done.3 = s32[1,16]{1,0:T(1,128)S(1)} copy-done((s32[1,16]{1,0:T(1,128)S(1)}, s32[1,16]{1,0:T(1,128)}, u32[]{:S(2)}) %copy-start.3) | copy-done | bytes 88
  1.6 0.0 copy-done.4
  1.6 0.0 copy-start
  1.7 1.0 %copy-done = f32[2,128,512]{2,1,0:T(8,128)S(1)} copy-done((f32[2,128,512]{2,1,0:T(8,128)S(1)}, f32[2,128,512]{2,1,0:T(8,128)}, u32[]{:S(2)}) %copy-start) | copy-done | bytes 524312
  2.7 0.0 copy-start.2
  2.7 0.9 %copy-done.2 = bf16[256,384]{1,0:T(8,128)(2,1)S(1)} copy-done((bf16[256,384]{1,0:T(8,128)(2,1)S(1)}, bf16[256,384]{1,0:T(8,128)(2,1)}, u32[]{:S(2)}) %copy-start.2) | copy-done | bytes 196632
  3.6 29.6 %shard_map.64 = f32[16,8192]{1,0:T(8,128)S(1)} custom-call(s32[1,16]{1,0:T(1,128)S(1)} %copy-done.3, s32[16]{0:T(128)S(1)} %copy-done.4, bf16[2,64,512]{2,1,0:T(8,128)(2,1)S(1)} %bitcast.7, bf16[256,384]{1,0:T(8,128)(2,1)S(1)} %copy-done.2, f32[2,128,512]{2,1,0:T(8,128)S(1)} %copy-done, bf16[128,1024]{1,0:T(8,128)(2,1)S(1)} %copy-done.1), custom_call_target="tpu_custom_call" | custom-call | tf_op jit(solution)/shard_map/pallas_call | solution.py:299
  33.3 0.8 %copy.11 = f32[1,16,8192]{2,1,0:T(8,128)} copy(f32[1,16,8192]{2,1,0:T(8,128)S(1)} %bitcast.6) | data formatting | bytes 1048576
Async XLA Ops:
  0.0 1.0 %copy-start.1 = (bf16[128,1024]{1,0:T(8,128)(2,1)S(1)}, bf16[128,1024]{1,0:T(8,128)(2,1)}, u32[]{:S(2)}) copy-start(bf16[128,1024]{1,0:T(8,128)(2,1)} %constant.8.clone.two_ref) | copy-start | bytes 786436
  1.0 0.7 %copy-start.3 = (s32[1,16]{1,0:T(1,128)S(1)}, s32[1,16]{1,0:T(1,128)}, u32[]{:S(2)}) copy-start(s32[1,16]{1,0:T(1,128)} %mask_ref.1) | copy-start | bytes 196
  1.0 0.7 %copy-start.4 = (s32[16]{0:T(128)S(1)}, s32[16]{0:T(128)}, u32[]{:S(2)}) copy-start(s32[16]{0:T(128)} %avail_ref.1) | copy-start | bytes 196
  1.6 1.0 %copy-start = (f32[2,128,512]{2,1,0:T(8,128)S(1)}, f32[2,128,512]{2,1,0:T(8,128)}, u32[]{:S(2)}) copy-start(f32[2,128,512]{2,1,0:T(8,128)} %constant.7.clone.twist_ref) | copy-start | bytes 1572868
  2.7 0.9 %copy-start.2 = (bf16[256,384]{1,0:T(8,128)(2,1)S(1)}, bf16[256,384]{1,0:T(8,128)(2,1)}, u32[]{:S(2)}) copy-start(bf16[256,384]{1,0:T(8,128)(2,1)} %constant.6.clone.one_ref) | copy-start | bytes 589828

commit v2 on v1

--- a/solution.py
+++ b/solution.py
@@ -12,6 +12,7 @@
 LAGS = 8192
 MESH = pl.DeviceIdType.MESH
 PIECES = 2
+DETOUR = 1
 LINE = 2
 CORES = 2
 
@@ -58,10 +59,14 @@
     mask_ref,
     avail_ref,
     x_ref,
+    one_hbm,
+    twist_hbm,
+    two_hbm,
+    out_ref,
     one_ref,
     twist_ref,
     two_ref,
-    out_ref,
+    table_sem,
     buf,
     own,
     res,
@@ -117,6 +122,9 @@
     def over(p, k, mine=False):
         return copy(index(p, side, core), p, k, send_d.at[0, p, k], 2, twin, mine)
 
+    def down_side(k):
+        return copy(index(plane, 1 - side, core), plane, k, send_x.at[plane, k], 1, below)
+
     def over_side(p, k):
         return copy(index(p, 1 - side, core), p, k, send_d.at[1, p, k], 3, twin)
 
@@ -131,6 +139,12 @@
             device_id_type=MESH,
         ).wait_recv()
 
+    loads = [
+        pltpu.make_async_copy(source, target, table_sem.at[n])
+        for n, (source, target) in enumerate(
+            ((one_hbm, one_ref), (twist_hbm, twist_ref), (two_hbm, two_ref))
+        )
+    ]
     barrier = pltpu.get_barrier_semaphore()
     greet(beside)
     greet(twin)
@@ -142,6 +156,26 @@
     @pl.when(plane < planes - 1)
     def _():
         greet(above)
+
+    for load in loads:
+        load.start()
+
+    peers = 2 + jnp.where(plane > 0, 1, 0) + jnp.where(plane < planes - 1, 1, 0)
+    pl.semaphore_wait(barrier, peers)
+
+    for k in range(PIECES):
+
+        @pl.when(plane > 0)
+        def _():
+            down(plane, k, True).start()
+
+        @pl.when(side == 1)
+        def _():
+            across(plane, k, True).start()
+
+        @pl.when(core == 1)
+        def _():
+            over(plane, k, True).start()
 
     first = (
         (lax.broadcasted_iota(jnp.int32, (depth, x_ref.shape[2]), 0) == 0)
@@ -150,23 +184,6 @@
     weight = jnp.where(first, 0.5, 1.0)
     own[0] = x_ref[0].astype(jnp.float32) * weight
     own[1] = x_ref[1].astype(jnp.float32) * weight
-
-    peers = 2 + jnp.where(plane > 0, 1, 0) + jnp.where(plane < planes - 1, 1, 0)
-    pl.semaphore_wait(barrier, peers)
-
-    for k in range(PIECES):
-
-        @pl.when(plane > 0)
-        def _():
-            down(plane, k, True).start()
-
-        @pl.when(side == 1)
-        def _():
-            across(plane, k, True).start()
-
-        @pl.when(core == 1)
-        def _():
-            over(plane, k, True).start()
 
     def clear(g, carry):
         res[g] = jnp.zeros(res.shape[1:], jnp.float32)
@@ -199,29 +216,7 @@
         flag = (mask_ref[0, station] * avail_ref[me] * avail_ref[station]).astype(jnp.float32)
         res[station] = total * (flag * scale)
 
-    def side_in(p):
-        for k in range(PIECES):
-            arrived(index(p, 1 - side, core), p, k, 1)
-            over_side(p, k).start()
-
-    @pl.when(side == 0)
-    def _():
-        side_in(plane)
-
-    @pl.when(core == 0)
-    def _():
-        for k in range(PIECES):
-            arrived(twin, plane, k, 2)
-        correlate(twin)
-
-    @pl.when(side == 0)
-    def _():
-        correlate(beside)
-        for k in range(PIECES):
-            arrived(index(plane, 1 - side, 1 - core), plane, k, 3)
-        correlate(index(plane, 1 - side, 1 - core))
-
-    def step(p, carry):
+    def column_in(p):
         for k in range(PIECES):
             arrived(index(p, side, core), p, k, 0)
 
@@ -229,20 +224,66 @@
             def _():
                 down(p, k).start()
 
-            across(p, k).start()
+            if k < DETOUR:
+
+                @pl.when((side == 0) | (p > plane + 1))
+                def _():
+                    across(p, k).start()
+
+            else:
+                across(p, k).start()
             over(p, k).start()
-        correlate(index(p, side, core))
-        side_in(p)
+
+    def side_in(p):
+        for k in range(PIECES):
+            arrived(index(p, 1 - side, core), p, k, 1)
+            over_side(p, k).start()
+            if k < DETOUR:
+
+                @pl.when((p == plane) & (plane > 0))
+                def _():
+                    down_side(k).start()
+
+    def twin_column(p):
         for k in range(PIECES):
             arrived(index(p, side, 1 - core), p, k, 2)
         correlate(index(p, side, 1 - core))
+
+    def twin_side(p):
         correlate(index(p, 1 - side, core))
         for k in range(PIECES):
             arrived(index(p, 1 - side, 1 - core), p, k, 3)
         correlate(index(p, 1 - side, 1 - core))
+
+    for load in loads:
+        load.wait()
+
+    @pl.when(core == 0)
+    def _():
+        twin_column(plane)
+
+    def step(p, carry):
+        column_in(p)
+        correlate(index(p, side, core))
+
+        @pl.when((side == 0) | (p > plane + 1))
+        def _():
+            side_in(p - 1)
+
+        twin_column(p)
+
+        @pl.when((side == 0) | (p > plane + 1))
+        def _():
+            twin_side(p - 1)
+
         return carry
 
     lax.fori_loop(plane + 1, planes, step, 0)
+
+    @pl.when((side == 0) | (plane < planes - 1))
+    def _():
+        side_in(planes - 1)
+        twin_side(planes - 1)
 
     group = math.gcd(devices, 8)
 
@@ -268,6 +309,12 @@
         def _():
             over_side(plane, k).wait_send()
 
+        if k < DETOUR:
+
+            @pl.when((side == 0) & (plane > 0))
+            def _():
+                down_side(k).wait_send()
+
         @pl.when(core == 1)
         def _():
             over(plane, k, True).wait_send()
@@ -279,7 +326,14 @@
             def _():
                 down(p, k).wait_send()
 
-            across(p, k).wait_send()
+            if k < DETOUR:
+
+                @pl.when((side == 0) | (p > plane + 1))
+                def _():
+                    across(p, k).wait_send()
+
+            else:
+                across(p, k).wait_send()
             over(p, k).wait_send()
             over_side(p, k).wait_send()
         return carry
@@ -295,13 +349,18 @@
     depth = freq // column
     planes = devices // (LINE * CORES)
     vmem = pl.BlockSpec(memory_space=pltpu.VMEM)
+    hbm = pl.BlockSpec(memory_space=pltpu.HBM)
     smem = pl.BlockSpec(memory_space=pltpu.SMEM)
     rows = pl.pallas_call(
         functools.partial(kernel, devices),
         out_shape=jax.ShapeDtypeStruct((devices, LAGS), jnp.float32),
-        in_specs=[smem, smem, vmem, vmem, vmem, vmem],
+        in_specs=[smem, smem, vmem, hbm, hbm, hbm],
         out_specs=vmem,
         scratch_shapes=[
+            pltpu.VMEM(one.shape, jnp.bfloat16),
+            pltpu.VMEM(twist.shape, jnp.float32),
+            pltpu.VMEM(two.shape, jnp.bfloat16),
+            pltpu.SemaphoreType.DMA((3,)),
             pltpu.VMEM((devices, 2, depth, column), jnp.bfloat16),
             pltpu.VMEM((2, depth, column), jnp.float32),
             pltpu.VMEM((devices, LAGS // inner, inner), jnp.float32),

time: 34.3 us -> 28.5 us (0.83)
  the two profiles are of different devices: /device:TPU:3 before, /device:TPU:1 now
where the time goes in v2:
time: 28.5 us; the launch traced here: 28.3 us
  Pallas kernels  23.9 us (84%)
  local copies, waits for them, and re-layouts  4.39 us (15%)
    pallas_call x1, Pallas kernels, per_device(): pl.pallas_call(functools.partial(kernel, devices), out_shape=jax.ShapeDty...  23.9 us
    unnamed x12, local copies, waits for them, and re-layouts  4.39 us

profile of v2, /device:TPU:1, one launch (start us, length us, event | category | flops | bytes accessed | tf_op | source)
XLA Modules:
  0.0 28.3 jit_solution(169996118216266072)
XLA Ops:
  0.0 0.0 copy-start.1
  0.0 1.0 %copy.9 = bf16[1,2,64,512]{3,2,1,0:T(8,128)(2,1)S(1)} copy(bf16[1,2,64,512]{3,1,2,0:T(2,128)(2,1)} %bitcast.8) | data formatting | bytes 262144
  1.0 0.0 copy-start.3
  1.0 0.0 copy-start.4
  1.0 0.0 copy-done.1
  1.0 0.6 %copy-done.3 = s32[1,16]{1,0:T(1,128)S(1)} copy-done((s32[1,16]{1,0:T(1,128)S(1)}, s32[1,16]{1,0:T(1,128)}, u32[]{:S(2)}) %copy-start.3) | copy-done | bytes 88
  1.6 0.0 copy-done.4
  1.6 0.0 copy-start
  1.7 1.0 %copy-done = f32[2,128,512]{2,1,0:T(8,128)S(1)} copy-done((f32[2,128,512]{2,1,0:T(8,128)S(1)}, f32[2,128,512]{2,1,0:T(8,128)}, u32[]{:S(2)}) %copy-start) | copy-done | bytes 524312
  2.7 0.0 copy-start.2
  2.7 0.9 %copy-done.2 = bf16[256,384]{1,0:T(8,128)(2,1)S(1)} copy-done((bf16[256,384]{1,0:T(8,128)(2,1)S(1)}, bf16[256,384]{1,0:T(8,128)(2,1)}, u32[]{:S(2)}) %copy-start.2) | copy-done | bytes 196632
  3.6 23.9 %shard_map.64 = f32[16,8192]{1,0:T(8,128)S(1)} custom-call(s32[1,16]{1,0:T(1,128)S(1)} %copy-done.3, s32[16]{0:T(128)S(1)} %copy-done.4, bf16[2,64,512]{2,1,0:T(8,128)(2,1)S(1)} %bitcast.7, bf16[256,384]{1,0:T(8,128)(2,1)S(1)} %copy-done.2, f32[2,128,512]{2,1,0:T(8,128)S(1)} %copy-done, bf16[128,1024]{1,0:T(8,128)(2,1)S(1)} %copy-done.1), custom_call_target="tpu_custom_call" | custom-call | tf_op jit(solution)/shard_map/pallas_call | solution.py:354
  27.5 0.8 %copy.11 = f32[1,16,8192]{2,1,0:T(8,128)} copy(f32[1,16,8192]{2,1,0:T(8,128)S(1)} %bitcast.6) | data formatting | bytes 1048576
Async XLA Ops:
  0.0 1.0 %copy-start.1 = (bf16[128,1024]{1,0:T(8,128)(2,1)S(1)}, bf16[128,1024]{1,0:T(8,128)(2,1)}, u32[]{:S(2)}) copy-start(bf16[128,1024]{1,0:T(8,128)(2,1)} %constant.8.clone.two_hbm) | copy-start | bytes 786436
  1.0 0.7 %copy-start.3 = (s32[1,16]{1,0:T(1,128)S(1)}, s32[1,16]{1,0:T(1,128)}, u32[]{:S(2)}) copy-start(s32[1,16]{1,0:T(1,128)} %mask_ref.1) | copy-start | bytes 196
  1.0 0.7 %copy-start.4 = (s32[16]{0:T(128)S(1)}, s32[16]{0:T(128)}, u32[]{:S(2)}) copy-start(s32[16]{0:T(128)} %avail_ref.1) | copy-start | bytes 196
  1.6 1.0 %copy-start = (f32[2,128,512]{2,1,0:T(8,128)S(1)}, f32[2,128,512]{2,1,0:T(8,128)}, u32[]{:S(2)}) copy-start(f32[2,128,512]{2,1,0:T(8,128)} %constant.7.clone.twist_hbm) | copy-start | bytes 1572868
  2.7 0.9 %copy-start.2 = (bf16[256,384]{1,0:T(8,128)(2,1)S(1)}, bf16[256,384]{1,0:T(8,128)(2,1)}, u32[]{:S(2)}) copy-start(bf16[256,384]{1,0:T(8,128)(2,1)} %constant.6.clone.one_hbm) | copy-start | bytes 589828

commit v3 on v2

--- a/solution.py
+++ b/solution.py
@@ -15,6 +15,7 @@
 DETOUR = 1
 LINE = 2
 CORES = 2
+GRANT = 67_043_328
 
 
 def split(value):
@@ -370,7 +371,7 @@
             pltpu.SemaphoreType.DMA((2, planes, PIECES)),
         ],
         compiler_params=pltpu.CompilerParams(
-            collective_id=0, has_side_effects=True, vmem_limit_bytes=48 * 1024 * 1024
+            collective_id=0, has_side_effects=True, vmem_limit_bytes=GRANT
         ),
     )(
         pair_mask,

time: 28.5 us -> 28.7 us (level)
  Pallas kernels: 23.9 us -> 25.1 us
  local copies, waits for them, and re-layouts: 4.39 us -> 3.44 us
    pallas_call x1, Pallas kernels: 23.9 us -> 25.1 us  [per_device(): pl.pallas_call(functools.partial(kernel, devices), out_shape=jax.ShapeDty...]
    unnamed x12 -> x2, local copies, waits for them, and re-layouts: 4.39 us -> 3.44 us
where the time goes in v3:
time: 28.7 us; the launch traced here: 28.5 us
  Pallas kernels  25.1 us (87%)
  local copies, waits for them, and re-layouts  3.44 us (12%)
    pallas_call x1, Pallas kernels, per_device(): pl.pallas_call(functools.partial(kernel, devices), out_shape=jax.ShapeDty...  25.1 us
    unnamed x2, local copies, waits for them, and re-layouts  3.44 us

profile of v3, /device:TPU:1, one launch (start us, length us, event | category | flops | bytes accessed | tf_op | source)
XLA Modules:
  0.0 28.5 jit_solution(12664494237217736938)
XLA Ops:
  0.0 1.6 %copy.9 = bf16[1,2,64,512]{3,2,1,0:T(8,128)(2,1)} copy(bf16[1,2,64,512]{3,1,2,0:T(2,128)(2,1)} %bitcast.8) | data formatting | bytes 262144
  1.6 25.1 %shard_map.64 = f32[16,8192]{1,0:T(8,128)} custom-call(s32[1,16]{1,0:T(1,128)} %mask_ref.1, s32[16]{0:T(128)} %avail_ref.1, bf16[2,64,512]{2,1,0:T(8,128)(2,1)} %bitcast.7, bf16[256,384]{1,0:T(8,128)(2,1)} %constant.6.clone.one_hbm, f32[2,128,512]{2,1,0:T(8,128)} %constant.7.clone.twist_hbm, bf16[128,1024]{1,0:T(8,128)(2,1)} %constant.8.clone.two_hbm), custom_call_target="tpu_custom_call" | custom-call | tf_op jit(solution)/shard_map/pallas_call | solution.py:355
  26.7 1.9 %copy.11 = f32[1,16,8192]{2,1,0:T(8,128)} copy(f32[1,16,8192]{2,1,0:T(8,128)} %bitcast.6) | data formatting | bytes 1048576

commit v4 on v2

--- a/solution.py
+++ b/solution.py
@@ -11,10 +11,11 @@
 
 LAGS = 8192
 MESH = pl.DeviceIdType.MESH
-PIECES = 2
-DETOUR = 1
+PIECES = 4
+DETOUR = 2
 LINE = 2
 CORES = 2
+LANES = 128
 
 
 def split(value):
@@ -40,18 +41,12 @@
     second = turn * ((np.arange(outer)[:, None] * k_column) % column) / column
     two = np.concatenate([np.cos(second), -np.sin(second)], axis=1).astype(np.float32)
 
-    def halves(table):
-        high = table.astype(jnp.bfloat16)
-        low = (table - high.astype(np.float32)).astype(jnp.bfloat16)
-        return high, low
-
-    one_high, one_low = halves(one)
-    two_high, two_low = halves(two)
-    return (
-        np.concatenate([one_high, one_high, one_low], axis=1),
-        np.stack([np.cos(twist), np.sin(twist)]).astype(np.float32),
-        np.concatenate([two_high, two_low], axis=0),
-    )
+    def stacked(table):
+        return np.concatenate(np.split(table, table.shape[1] // LANES, axis=1), axis=0)
+
+    turns = [np.cos(twist).astype(np.float32), np.sin(twist).astype(np.float32)]
+    packed = np.concatenate([stacked(part) for part in (*turns, one, two)], axis=0)
+    return packed, inner, column, outer
 
 
 def kernel(
@@ -59,14 +54,11 @@
     mask_ref,
     avail_ref,
     x_ref,
-    one_hbm,
-    twist_hbm,
-    two_hbm,
+    packed_ref,
     out_ref,
     one_ref,
     twist_ref,
     two_ref,
-    table_sem,
     buf,
     own,
     res,
@@ -81,12 +73,11 @@
     chip = me // CORES
     side = chip % LINE
     plane = chip // LINE
-    depth = x_ref.shape[1]
+    depth, column = x_ref.shape[1:]
+    rows = depth // PIECES
     inner = twist_ref.shape[1]
     outer = two_ref.shape[0] // 2
-    freq = depth * x_ref.shape[2]
-    scale = 2.0 / math.sqrt(8.0 * freq)
-    rows = depth // PIECES
+    scale = 2.0 / math.sqrt(8.0 * depth * column)
 
     def index(p, s, c):
         return (p * LINE + s) * CORES + c
@@ -99,13 +90,10 @@
     def greet(device):
         pl.semaphore_signal(barrier, inc=1, device_id={"row": device}, device_id_type=MESH)
 
-    def piece(ref, k):
-        return ref.at[:, pl.ds(k * rows, rows), :]
-
     def copy(station, p, k, sem, kind, device, mine=False):
-        slot = piece(buf.at[station], k)
+        slot = buf.at[station, k]
         return pltpu.make_async_remote_copy(
-            src_ref=piece(x_ref, k) if mine else slot,
+            src_ref=x_ref.at[:, pl.ds(k * rows, rows), :] if mine else slot,
             dst_ref=slot,
             send_sem=sem,
             recv_sem=recv.at[kind, p, k],
@@ -129,7 +117,7 @@
         return copy(index(p, 1 - side, core), p, k, send_d.at[1, p, k], 3, twin)
 
     def arrived(station, p, k, kind):
-        slot = piece(buf.at[station], k)
+        slot = buf.at[station, k]
         pltpu.make_async_remote_copy(
             src_ref=slot,
             dst_ref=slot,
@@ -139,12 +127,6 @@
             device_id_type=MESH,
         ).wait_recv()
 
-    loads = [
-        pltpu.make_async_copy(source, target, table_sem.at[n])
-        for n, (source, target) in enumerate(
-            ((one_hbm, one_ref), (twist_hbm, twist_ref), (two_hbm, two_ref))
-        )
-    ]
     barrier = pltpu.get_barrier_semaphore()
     greet(beside)
     greet(twin)
@@ -157,9 +139,6 @@
     def _():
         greet(above)
 
-    for load in loads:
-        load.start()
-
     peers = 2 + jnp.where(plane > 0, 1, 0) + jnp.where(plane < planes - 1, 1, 0)
     pl.semaphore_wait(barrier, peers)
 
@@ -178,13 +157,30 @@
             over(plane, k, True).start()
 
     first = (
-        (lax.broadcasted_iota(jnp.int32, (depth, x_ref.shape[2]), 0) == 0)
-        & (lax.broadcasted_iota(jnp.int32, (depth, x_ref.shape[2]), 1) == 0)
+        (lax.broadcasted_iota(jnp.int32, (depth, column), 0) == 0)
+        & (lax.broadcasted_iota(jnp.int32, (depth, column), 1) == 0)
     )
     weight = jnp.where(first, 0.5, 1.0)
     own[0] = x_ref[0].astype(jnp.float32) * weight
     own[1] = x_ref[1].astype(jnp.float32) * weight
 
+    at = 0
+    for part in range(2):
+        for b in range(column // LANES):
+            twist_ref[part, :, b * LANES : (b + 1) * LANES] = packed_ref[at : at + inner, :]
+            at += inner
+    for b in range(2 * depth // LANES):
+        high, low = split(packed_ref[at : at + 2 * inner, :])
+        for n, term in enumerate((high, high, low)):
+            left = 2 * depth * n + b * LANES
+            one_ref[:, left : left + LANES] = term
+        at += 2 * inner
+    for b in range(2 * column // LANES):
+        high, low = split(packed_ref[at : at + outer, :])
+        two_ref[:outer, b * LANES : (b + 1) * LANES] = high
+        two_ref[outer:, b * LANES : (b + 1) * LANES] = low
+        at += outer
+
     def clear(g, carry):
         res[g] = jnp.zeros(res.shape[1:], jnp.float32)
         return carry
@@ -193,8 +189,8 @@
 
     def correlate(station):
         own_re, own_im = own[0], own[1]
-        re = buf[station, 0].astype(jnp.float32)
-        im = buf[station, 1].astype(jnp.float32)
+        re = buf[station, :, 0].astype(jnp.float32).reshape(depth, column)
+        im = buf[station, :, 1].astype(jnp.float32).reshape(depth, column)
         re_high, re_low = split(own_re * re + own_im * im)
         im_high, im_low = split(own_re * im - own_im * re)
         cross = jnp.concatenate([re_high, im_high, re_low, im_low, re_high, im_high], axis=0)
@@ -216,65 +212,68 @@
         flag = (mask_ref[0, station] * avail_ref[me] * avail_ref[station]).astype(jnp.float32)
         res[station] = total * (flag * scale)
 
-    def column_in(p):
-        for k in range(PIECES):
-            arrived(index(p, side, core), p, k, 0)
-
-            @pl.when(plane > 0)
-            def _():
-                down(p, k).start()
-
-            if k < DETOUR:
-
-                @pl.when((side == 0) | (p > plane + 1))
-                def _():
-                    across(p, k).start()
-
-            else:
+    def column_in(p, k):
+        arrived(index(p, side, core), p, k, 0)
+
+        @pl.when(plane > 0)
+        def _():
+            down(p, k).start()
+
+        if k < DETOUR:
+
+            @pl.when((side == 0) | (p > plane + 1))
+            def _():
                 across(p, k).start()
-            over(p, k).start()
-
-    def side_in(p):
-        for k in range(PIECES):
-            arrived(index(p, 1 - side, core), p, k, 1)
-            over_side(p, k).start()
-            if k < DETOUR:
-
-                @pl.when((p == plane) & (plane > 0))
-                def _():
-                    down_side(k).start()
-
-    def twin_column(p):
+
+        else:
+            across(p, k).start()
+        over(p, k).start()
+
+    def side_in(p, k):
+        arrived(index(p, 1 - side, core), p, k, 1)
+        over_side(p, k).start()
+        if k < DETOUR:
+
+            @pl.when((p == plane) & (plane > 0))
+            def _():
+                down_side(k).start()
+
+    def twin_column_in(p):
         for k in range(PIECES):
             arrived(index(p, side, 1 - core), p, k, 2)
-        correlate(index(p, side, 1 - core))
-
-    def twin_side(p):
-        correlate(index(p, 1 - side, core))
+
+    def twin_side_in(p):
         for k in range(PIECES):
             arrived(index(p, 1 - side, 1 - core), p, k, 3)
-        correlate(index(p, 1 - side, 1 - core))
-
-    for load in loads:
-        load.wait()
 
     @pl.when(core == 0)
     def _():
-        twin_column(plane)
+        twin_column_in(plane)
+        correlate(twin)
 
     def step(p, carry):
-        column_in(p)
-        correlate(index(p, side, core))
-
-        @pl.when((side == 0) | (p > plane + 1))
-        def _():
-            side_in(p - 1)
-
-        twin_column(p)
-
-        @pl.when((side == 0) | (p > plane + 1))
-        def _():
-            twin_side(p - 1)
+        both = (side == 0) | (p > plane + 1)
+        for k in range(PIECES):
+            column_in(p, k)
+
+            @pl.when(both)
+            def _():
+                side_in(p - 1, k)
+
+        @pl.when(both)
+        def _():
+            correlate(index(p, side, core))
+            correlate(index(p - 1, 1 - side, core))
+            twin_column_in(p)
+            twin_side_in(p - 1)
+            correlate(index(p, side, 1 - core))
+            correlate(index(p - 1, 1 - side, 1 - core))
+
+        @pl.when(jnp.logical_not(both))
+        def _():
+            correlate(index(p, side, core))
+            twin_column_in(p)
+            correlate(index(p, side, 1 - core))
 
         return carry
 
@@ -282,8 +281,11 @@
 
     @pl.when((side == 0) | (plane < planes - 1))
     def _():
-        side_in(planes - 1)
-        twin_side(planes - 1)
+        for k in range(PIECES):
+            side_in(planes - 1, k)
+        correlate(index(planes - 1, 1 - side, core))
+        twin_side_in(planes - 1)
+        correlate(index(planes - 1, 1 - side, 1 - core))
 
     group = math.gcd(devices, 8)
 
@@ -344,26 +346,24 @@
 def per_device(spectra, pair_mask, available):
     devices = lax.axis_size("row")
     freq = spectra.shape[2]
-    one, twist, two = build_tables(freq, LAGS)
-    inner, column = twist.shape[1:]
+    packed, inner, column, outer = build_tables(freq, LAGS)
     depth = freq // column
     planes = devices // (LINE * CORES)
+    shape = (PIECES, 2, depth // PIECES, column)
     vmem = pl.BlockSpec(memory_space=pltpu.VMEM)
-    hbm = pl.BlockSpec(memory_space=pltpu.HBM)
     smem = pl.BlockSpec(memory_space=pltpu.SMEM)
     rows = pl.pallas_call(
         functools.partial(kernel, devices),
         out_shape=jax.ShapeDtypeStruct((devices, LAGS), jnp.float32),
-        in_specs=[smem, smem, vmem, hbm, hbm, hbm],
+        in_specs=[smem, smem, vmem, vmem],
         out_specs=vmem,
         scratch_shapes=[
-            pltpu.VMEM(one.shape, jnp.bfloat16),
-            pltpu.VMEM(twist.shape, jnp.float32),
-            pltpu.VMEM(two.shape, jnp.bfloat16),
-            pltpu.SemaphoreType.DMA((3,)),
-            pltpu.VMEM((devices, 2, depth, column), jnp.bfloat16),
+            pltpu.VMEM((2 * inner, 3 * 2 * depth), jnp.bfloat16),
+            pltpu.VMEM((2, inner, column), jnp.float32),
+            pltpu.VMEM((2 * outer, 2 * column), jnp.bfloat16),
+            pltpu.VMEM((devices, *shape), jnp.bfloat16),
             pltpu.VMEM((2, depth, column), jnp.float32),
-            pltpu.VMEM((devices, LAGS // inner, inner), jnp.float32),
+            pltpu.VMEM((devices, outer, inner), jnp.float32),
             pltpu.SemaphoreType.DMA((4, planes, PIECES)),
             pltpu.SemaphoreType.DMA((planes, PIECES)),
             pltpu.SemaphoreType.DMA((planes, PIECES)),
@@ -376,9 +376,7 @@
         pair_mask,
         available,
         spectra.reshape(2, depth, column),
-        jnp.asarray(one),
-        jnp.asarray(twist),
-        jnp.asarray(two),
+        jnp.asarray(packed),
     )
     return rows[None]
 

time: 28.5 us -> 27 us (0.947)
  local copies, waits for them, and re-layouts: 4.39 us -> 3.55 us
  Pallas kernels: 23.9 us -> 23.3 us
    unnamed x12 -> x8, local copies, waits for them, and re-layouts: 4.39 us -> 3.55 us
    pallas_call x1, Pallas kernels: 23.9 us -> 23.3 us  [per_device(): pl.pallas_call(functools.partial(kernel, devices), out_shape=jax.ShapeDty...]
where the time goes in v4:
time: 27 us; the launch traced here: 26.8 us
  Pallas kernels  23.3 us (86%)
  local copies, waits for them, and re-layouts  3.55 us (13%)
    pallas_call x1, Pallas kernels, per_device(): pl.pallas_call(functools.partial(kernel, devices), out_shape=jax.ShapeDty...  23.3 us
    unnamed x8, local copies, waits for them, and re-layouts  3.55 us

profile of v4, /device:TPU:1, one launch (start us, length us, event | category | flops | bytes accessed | tf_op | source)
XLA Modules:
  0.0 26.8 jit_solution(16845942330575313703)
XLA Ops:
  0.0 0.9 %copy.7 = bf16[1,2,64,512]{3,2,1,0:T(8,128)(2,1)S(1)} copy(bf16[1,2,64,512]{3,1,2,0:T(2,128)(2,1)} %bitcast.8) | data formatting | bytes 262144
  0.9 0.0 copy-start.1
  0.9 0.0 copy-start.2
  0.9 0.6 %copy-done.1 = s32[1,16]{1,0:T(1,128)S(1)} copy-done((s32[1,16]{1,0:T(1,128)S(1)}, s32[1,16]{1,0:T(1,128)}, u32[]{:S(2)}) %copy-start.1) | copy-done | bytes 88
  1.6 0.0 copy-done.2
  1.6 0.0 copy-start
  1.6 1.2 %copy-done = f32[1792,128]{1,0:T(8,128)S(1)} copy-done((f32[1792,128]{1,0:T(8,128)S(1)}, f32[1792,128]{1,0:T(8,128)}, u32[]{:S(2)}) %copy-start) | copy-done | bytes 917528
  2.8 23.3 %shard_map.46 = f32[16,8192]{1,0:T(8,128)S(1)} custom-call(s32[1,16]{1,0:T(1,128)S(1)} %copy-done.1, s32[16]{0:T(128)S(1)} %copy-done.2, bf16[2,64,512]{2,1,0:T(8,128)(2,1)S(1)} %bitcast.7, f32[1792,128]{1,0:T(8,128)S(1)} %copy-done), custom_call_target="tpu_custom_call" | custom-call | tf_op jit(solution)/shard_map/pallas_call | solution.py:355
  26.1 0.8 %copy.9 = f32[1,16,8192]{2,1,0:T(8,128)} copy(f32[1,16,8192]{2,1,0:T(8,128)S(1)} %bitcast.6) | data formatting | bytes 1048576
Async XLA Ops:
  0.9 0.7 %copy-start.1 = (s32[1,16]{1,0:T(1,128)S(1)}, s32[1,16]{1,0:T(1,128)}, u32[]{:S(2)}) copy-start(s32[1,16]{1,0:T(1,128)} %mask_ref.1) | copy-start | bytes 196
  0.9 0.7 %copy-start.2 = (s32[16]{0:T(128)S(1)}, s32[16]{0:T(128)}, u32[]{:S(2)}) copy-start(s32[16]{0:T(128)} %avail_ref.1) | copy-start | bytes 196
  1.6 1.2 %copy-start = (f32[1792,128]{1,0:T(8,128)S(1)}, f32[1792,128]{1,0:T(8,128)}, u32[]{:S(2)}) copy-start(f32[1792,128]{1,0:T(8,128)} %constant.2.clone.packed_ref) | copy-start | bytes 2752516

commit v5 on v4

--- a/solution.py
+++ b/solution.py
@@ -11,8 +11,8 @@
 
 LAGS = 8192
 MESH = pl.DeviceIdType.MESH
-PIECES = 4
-DETOUR = 2
+PIECES = 2
+DETOUR = 1
 LINE = 2
 CORES = 2
 LANES = 128
@@ -66,6 +66,7 @@
     send_z,
     send_x,
     send_d,
+    send_s,
 ):
     planes = devices // (LINE * CORES)
     me = lax.axis_index("row")
@@ -111,7 +112,8 @@
         return copy(index(p, side, core), p, k, send_d.at[0, p, k], 2, twin, mine)
 
     def down_side(k):
-        return copy(index(plane, 1 - side, core), plane, k, send_x.at[plane, k], 1, below)
+        p = planes - 1
+        return copy(index(p, 1 - side, core), p, k, send_s.at[k], 1, below)
 
     def over_side(p, k):
         return copy(index(p, 1 - side, core), p, k, send_d.at[1, p, k], 3, twin)
@@ -221,7 +223,7 @@
 
         if k < DETOUR:
 
-            @pl.when((side == 0) | (p > plane + 1))
+            @pl.when((side == 0) | (p < planes - 1))
             def _():
                 across(p, k).start()
 
@@ -234,7 +236,7 @@
         over_side(p, k).start()
         if k < DETOUR:
 
-            @pl.when((p == plane) & (plane > 0))
+            @pl.when((side == 0) & (plane > 0) & (p == planes - 1))
             def _():
                 down_side(k).start()
 
@@ -281,7 +283,7 @@
 
     @pl.when((side == 0) | (plane < planes - 1))
     def _():
-        for k in range(PIECES):
+        for k in reversed(range(PIECES)):
             side_in(planes - 1, k)
         correlate(index(planes - 1, 1 - side, core))
         twin_side_in(planes - 1)
@@ -330,7 +332,7 @@
 
             if k < DETOUR:
 
-                @pl.when((side == 0) | (p > plane + 1))
+                @pl.when((side == 0) | (p < planes - 1))
                 def _():
                     across(p, k).wait_send()
 
@@ -368,6 +370,7 @@
             pltpu.SemaphoreType.DMA((planes, PIECES)),
             pltpu.SemaphoreType.DMA((planes, PIECES)),
             pltpu.SemaphoreType.DMA((2, planes, PIECES)),
+            pltpu.SemaphoreType.DMA((DETOUR,)),
         ],
         compiler_params=pltpu.CompilerParams(
             collective_id=0, has_side_effects=True, vmem_limit_bytes=48 * 1024 * 1024

time: 27 us -> 26.2 us (0.970)
  Pallas kernels: 23.3 us -> 22.5 us
    pallas_call x1, Pallas kernels: 23.3 us -> 22.5 us  [per_device(): pl.pallas_call(functools.partial(kernel, devices), out_shape=jax.ShapeDty...]
where the time goes in v5:
time: 26.2 us; the launch traced here: 26.1 us
  Pallas kernels  22.5 us (86%)
  local copies, waits for them, and re-layouts  3.55 us (14%)
    pallas_call x1, Pallas kernels, per_device(): pl.pallas_call(functools.partial(kernel, devices), out_shape=jax.ShapeDty...  22.5 us
    unnamed x8, local copies, waits for them, and re-layouts  3.55 us

profile of v5, /device:TPU:1, one launch (start us, length us, event | category | flops | bytes accessed | tf_op | source)
XLA Modules:
  0.0 26.1 jit_solution(10859458442499482678)
XLA Ops:
  0.0 0.9 %copy.7 = bf16[1,2,64,512]{3,2,1,0:T(8,128)(2,1)S(1)} copy(bf16[1,2,64,512]{3,1,2,0:T(2,128)(2,1)} %bitcast.8) | data formatting | bytes 262144
  0.9 0.0 copy-start.1
  0.9 0.0 copy-start.2
  0.9 0.6 %copy-done.1 = s32[1,16]{1,0:T(1,128)S(1)} copy-done((s32[1,16]{1,0:T(1,128)S(1)}, s32[1,16]{1,0:T(1,128)}, u32[]{:S(2)}) %copy-start.1) | copy-done | bytes 88
  1.6 0.0 copy-done.2
  1.6 0.0 copy-start
  1.6 1.2 %copy-done = f32[1792,128]{1,0:T(8,128)S(1)} copy-done((f32[1792,128]{1,0:T(8,128)S(1)}, f32[1792,128]{1,0:T(8,128)}, u32[]{:S(2)}) %copy-start) | copy-done | bytes 917528
  2.8 22.5 %shard_map.46 = f32[16,8192]{1,0:T(8,128)S(1)} custom-call(s32[1,16]{1,0:T(1,128)S(1)} %copy-done.1, s32[16]{0:T(128)S(1)} %copy-done.2, bf16[2,64,512]{2,1,0:T(8,128)(2,1)S(1)} %bitcast.7, f32[1792,128]{1,0:T(8,128)S(1)} %copy-done), custom_call_target="tpu_custom_call" | custom-call | tf_op jit(solution)/shard_map/pallas_call | solution.py:357
  25.3 0.8 %copy.9 = f32[1,16,8192]{2,1,0:T(8,128)} copy(f32[1,16,8192]{2,1,0:T(8,128)S(1)} %bitcast.6) | data formatting | bytes 1048576
Async XLA Ops:
  0.9 0.7 %copy-start.1 = (s32[1,16]{1,0:T(1,128)S(1)}, s32[1,16]{1,0:T(1,128)}, u32[]{:S(2)}) copy-start(s32[1,16]{1,0:T(1,128)} %mask_ref.1) | copy-start | bytes 196
  0.9 0.7 %copy-start.2 = (s32[16]{0:T(128)S(1)}, s32[16]{0:T(128)}, u32[]{:S(2)}) copy-start(s32[16]{0:T(128)} %avail_ref.1) | copy-start | bytes 196
  1.6 1.2 %copy-start = (f32[1792,128]{1,0:T(8,128)S(1)}, f32[1792,128]{1,0:T(8,128)}, u32[]{:S(2)}) copy-start(f32[1792,128]{1,0:T(8,128)} %constant.2.clone.packed_ref) | copy-start | bytes 2752516

commit v6 on v5

--- a/solution.py
+++ b/solution.py
@@ -15,6 +15,7 @@
 DETOUR = 1
 LINE = 2
 CORES = 2
+GRANT = 55_250_000
 LANES = 128
 
 
@@ -54,7 +55,7 @@
     mask_ref,
     avail_ref,
     x_ref,
-    packed_ref,
+    packed_hbm,
     out_ref,
     one_ref,
     twist_ref,
@@ -67,6 +68,8 @@
     send_x,
     send_d,
     send_s,
+    packed_ref,
+    table_sem,
 ):
     planes = devices // (LINE * CORES)
     me = lax.axis_index("row")
@@ -129,6 +132,8 @@
             device_id_type=MESH,
         ).wait_recv()
 
+    load = pltpu.make_async_copy(packed_hbm, packed_ref, table_sem)
+    load.start()
     barrier = pltpu.get_barrier_semaphore()
     greet(beside)
     greet(twin)
@@ -166,6 +171,7 @@
     own[0] = x_ref[0].astype(jnp.float32) * weight
     own[1] = x_ref[1].astype(jnp.float32) * weight
 
+    load.wait()
     at = 0
     for part in range(2):
         for b in range(column // LANES):
@@ -357,7 +363,7 @@
     rows = pl.pallas_call(
         functools.partial(kernel, devices),
         out_shape=jax.ShapeDtypeStruct((devices, LAGS), jnp.float32),
-        in_specs=[smem, smem, vmem, vmem],
+        in_specs=[smem, smem, vmem, pl.BlockSpec(memory_space=pltpu.HBM)],
         out_specs=vmem,
         scratch_shapes=[
             pltpu.VMEM((2 * inner, 3 * 2 * depth), jnp.bfloat16),
@@ -371,9 +377,11 @@
             pltpu.SemaphoreType.DMA((planes, PIECES)),
             pltpu.SemaphoreType.DMA((2, planes, PIECES)),
             pltpu.SemaphoreType.DMA((DETOUR,)),
+            pltpu.VMEM(packed.shape, jnp.float32),
+            pltpu.SemaphoreType.DMA(()),
         ],
         compiler_params=pltpu.CompilerParams(
-            collective_id=0, has_side_effects=True, vmem_limit_bytes=48 * 1024 * 1024
+            collective_id=0, has_side_effects=True, vmem_limit_bytes=GRANT
         ),
     )(
         pair_mask,

time: 26.2 us -> 25 us (0.954)
  local copies, waits for them, and re-layouts: 3.55 us -> 2.37 us
    unnamed x8 -> x6, local copies, waits for them, and re-layouts: 3.55 us -> 2.37 us
where the time goes in v6:
time: 25 us; the launch traced here: 24.9 us
  Pallas kernels  22.5 us (90%)
  local copies, waits for them, and re-layouts  2.37 us (9%)
    pallas_call x1, Pallas kernels, per_device(): pl.pallas_call(functools.partial(kernel, devices), out_shape=jax.ShapeDty...  22.5 us
    unnamed x6, local copies, waits for them, and re-layouts  2.37 us

profile of v6, /device:TPU:1, one launch (start us, length us, event | category | flops | bytes accessed | tf_op | source)
XLA Modules:
  0.0 24.9 jit_solution(10395762537417002548)
XLA Ops:
  0.0 0.9 %copy.7 = bf16[1,2,64,512]{3,2,1,0:T(8,128)(2,1)S(1)} copy(bf16[1,2,64,512]{3,1,2,0:T(2,128)(2,1)} %bitcast.8) | data formatting | bytes 262144
  0.9 0.0 copy-start
  0.9 0.0 copy-start.1
  0.9 0.6 %copy-done = s32[1,16]{1,0:T(1,128)S(1)} copy-done((s32[1,16]{1,0:T(1,128)S(1)}, s32[1,16]{1,0:T(1,128)}, u32[]{:S(2)}) %copy-start) | copy-done | bytes 88
  1.6 0.0 copy-done.1
  1.6 22.5 %shard_map.46 = f32[16,8192]{1,0:T(8,128)S(1)} custom-call(s32[1,16]{1,0:T(1,128)S(1)} %copy-done, s32[16]{0:T(128)S(1)} %copy-done.1, bf16[2,64,512]{2,1,0:T(8,128)(2,1)S(1)} %bitcast.7, f32[1792,128]{1,0:T(8,128)} %constant.2.clone.packed_hbm), custom_call_target="tpu_custom_call" | custom-call | tf_op jit(solution)/shard_map/pallas_call | solution.py:363
  24.1 0.8 %copy.9 = f32[1,16,8192]{2,1,0:T(8,128)} copy(f32[1,16,8192]{2,1,0:T(8,128)S(1)} %bitcast.6) | data formatting | bytes 1048576
Async XLA Ops:
  0.9 0.7 %copy-start = (s32[1,16]{1,0:T(1,128)S(1)}, s32[1,16]{1,0:T(1,128)}, u32[]{:S(2)}) copy-start(s32[1,16]{1,0:T(1,128)} %mask_ref.1) | copy-start | bytes 196
  0.9 0.7 %copy-start.1 = (s32[16]{0:T(128)S(1)}, s32[16]{0:T(128)}, u32[]{:S(2)}) copy-start(s32[16]{0:T(128)} %avail_ref.1) | copy-start | bytes 196
